TPU v7x, 32 devices: a whole 2x2x4 slice. The times are simulated.
32 devices in a mesh: seq: 16 (over z, y, core), fsdp: 2 (over x).
Axes of the slice: x: 2, y: 2, z: 4, core: 2. Of those that a mesh axis runs over, the one named last changes fastest.
Arguments:
- tokens: bfloat16 [64, 8192], P('seq', 'fsdp'), may hold values from -6 to 6
- gate_weight: bfloat16 [8192, 16384], P('fsdp', 'seq'), may hold values from -0.0625 to 0.0625
- up_weight: bfloat16 [8192, 16384], P('fsdp', 'seq'), may hold values from -0.0625 to 0.0625
- down_weight: bfloat16 [8192, 16384], P('fsdp', 'seq'), may hold values from -0.046875 to 0.046875
Outputs:
- mixed_out: bfloat16 [64, 8192], P('seq', 'fsdp')
All inputs are finite; a program needn't handle non-finite values.
Results may differ from a plain program's by a relative error of at most 0.0049.
Values may be sent and summed in bfloat16 or wider, within the bound.
A program may use at most 64 MiB of HBM per device.

v0:
```python
import jax
import jax.numpy as jnp
from jax import lax
from jax.sharding import PartitionSpec as P


def project_down(hidden, weight):
    return lax.dot_general(
        hidden, weight, (((1,), (1,)), ((), ())), preferred_element_type=jnp.float32
    )


def on_device(tokens, gate_weight, up_weight, down_weight):
    units = gate_weight.shape[1]
    paired = jnp.concatenate([gate_weight, up_weight], axis=1)
    parts = jnp.dot(
        lax.all_gather(tokens, "seq", axis=0, tiled=True),
        paired,
        preferred_element_type=jnp.float32,
    )
    values = lax.psum(parts, "fsdp")
    hidden = (jax.nn.silu(values[:, :units]) * values[:, units:]).astype(jnp.bfloat16)
    return lax.psum_scatter(
        project_down(hidden, down_weight), "seq", scatter_dimension=0, tiled=True
    ).astype(jnp.bfloat16)


def solution(mesh):
    return jax.shard_map(
        on_device,
        mesh=mesh,
        in_specs=(P("seq", "fsdp"), P("fsdp", "seq"), P("fsdp", "seq"), P("fsdp", "seq")),
        out_specs=P("seq", "fsdp"),
        check_vma=False,
    )
```

profile of v0, /device:TPU:0, one launch (start us, length us, event | category | flops | bytes accessed | tf_op | source)
XLA Modules:
  0.0 152.2 jit_solution(14321686645150590111)
XLA Ops:
  6.5 0.0 all-reduce.4.cloned.1.call-start
  6.5 24.8 %all-gather = bf16[16,4,4096]{2,1,0:T(4,128)(2,1)S(1)} all-gather(bf16[1,4,4096]{2,1,0:T(4,128)(2,1)} %bitcast.6), channel_id=1, replica_groups=mesh['seq'=16,'fsdp'=2] {'seq'}, dimensions={0}, use_global_device_ids=true | all-gather | bytes 557056 | tf_op jit(solution)/shard_map/all_gather | solution.py:17
  31.3 0.1 reshape.1
  31.5 0.0 copy-start
  31.5 8.2 %fusion.4 = f32[64,2048]{1,0:T(8,128)} fusion(bf16[64,4096]{1,0:T(8,128)(2,1)S(1)} %reshape.1, bf16[4096,1024]{1,0:T(8,128)(2,1)} %param.6, bf16[4096,1024]{1,0:T(8,128)(2,1)} %param.5), kind=kOutput, calls=%fused_computation.4 | convolution fusion | flops 1107296256 | bytes 17825792 | tf_op jit(solution)/shard_map/dot_general | solution.py:16
  39.7 0.0 all-reduce.4.cloned.1.call-update
  39.8 0.0 copy-done
  39.8 0.6 dynamic-slice
  41.0 24.8 %all-reduce.4.cloned.1.call-done = f32[64,2048]{1,0:T(8,128)} async-done(((f32[64,2048]{1,0:T(8,128)}), f32[64,2048]{1,0:T(8,128)}) %all-reduce.4.cloned.1.call-update) | async-done | bytes 524304 | tf_op jit(solution)/shard_map/psum | solution.py:21
  65.8 6.2 %fusion.8 = f32[64,4096]{1,0:T(8,128)S(1)} fusion(bf16[4096,1024]{1,0:T(8,128)(2,1)} %param.7, f32[64,2048]{1,0:T(8,128)} %all-reduce.4.cloned.1.call-done), kind=kOutput, calls=%fused_computation.7 | convolution fusion | flops 537264128 | bytes 9961472 | tf_op jit(solution)/shard_map/dot_general | solution.py:8
  72.0 72.7 %all-reduce.5 = bf16[64,4096]{1,0:T(8,128)(2,1)S(1)} all-reduce(f32[64,4096]{1,0:T(8,128)S(1)} %fusion.8), channel_id=2, replica_groups=mesh['seq'=16,'fsdp'=2] {'seq'}, use_global_device_ids=true, to_apply=%region_1.2.clone | all-reduce | flops 262144 | bytes 1572864
  144.7 0.6 dynamic-slice_convert_fusion
Async XLA Ops:
  6.5 59.3 %all-reduce.4.cloned.1.call-start = ((), (), s32[]{:S(2)}) async-start(), calls=%async_computation | async-start | bytes 1048576 | tf_op jit(solution)/shard_map/psum | solution.py:21
  31.5 8.3 %copy-start = (u32[32]{0:T(128)S(1)}, u32[32]{0:T(128)}, u32[]{:S(2)}) copy-start(u32[32]{0:T(128)} %constant.6) | copy-start | bytes 388
Sparse Core Ops, SparseCore 0:
  39.9 25.8 all-reduce.3
where the time goes:
time: 152 us
  blocking collectives  97.5 us (64%)
  waiting for transfers between devices  24.8 us (16%)
  matrix products  14.5 us (10%)
  between operations  14.1 us (9%)
    unnamed x1, blocking collectives  72.7 us
    all_gather x1, blocking collectives, on_device(): lax.all_gather(tokens, 'seq', axis=0, tiled=True)  24.8 us
    psum x1, waiting for transfers between devices, on_device(): values = lax.psum(parts, 'fsdp')  24.8 us
    dot_general x1, matrix products, on_device(): jnp.dot(lax.all_gather(tokens, 'seq', axis=0, tiled=True), paired, prefer...  8.25 us
    dot_general x1, matrix products, project_down(): lax.dot_general(hidden, weight, (((1,), (1,)), ((), ())), preferred_eleme...  6.22 us
  transfers between devices with their start and end apart: 1, of which 1 were waited for; matrix products, arithmetic and copies ran while one was open for 0% of the time, Pallas kernels for 0%

commit v1 on v0

--- a/solution.py
+++ b/solution.py
@@ -2,6 +2,11 @@
 import jax.numpy as jnp
 from jax import lax
 from jax.sharding import PartitionSpec as P
+from jax.lax import all_gather
+
+
+def guide_the_types(chunk, along_axis):
+    return all_gather(chunk, along_axis).sum(axis=0)
 
 
 def project_down(hidden, weight):
@@ -18,7 +23,7 @@
         paired,
         preferred_element_type=jnp.float32,
     )
-    values = lax.psum(parts, "fsdp")
+    values = guide_the_types(parts, "fsdp")
     hidden = (jax.nn.silu(values[:, :units]) * values[:, units:]).astype(jnp.bfloat16)
     return lax.psum_scatter(
         project_down(hidden, down_weight), "seq", scatter_dimension=0, tiled=True

time: 152 us -> 146 us (0.961)
  waiting for transfers between devices: 24.8 us -> 17.5 us
    psum x1 -> x0, waiting for transfers between devices: 24.8 us -> none  [on_device(): values = lax.psum(parts, 'fsdp')]
    all_gather x0 -> x1, waiting for transfers between devices: none -> 17.4 us  [guide_the_types(): return all_gather(chunk, along_axis).sum(axis=0)]
where the time goes in v1:
time: 146 us
  blocking collectives  97.5 us (67%)
  waiting for transfers between devices  17.5 us (12%)
  matrix products  14.3 us (10%)
  between operations  14.1 us (10%)
    unnamed x1, blocking collectives  72.7 us
    all_gather x1, blocking collectives, on_device(): lax.all_gather(tokens, 'seq', axis=0, tiled=True)  24.8 us
    all_gather x1, waiting for transfers between devices, guide_the_types(): return all_gather(chunk, along_axis).sum(axis=0)  17.4 us
    dot_general x1, matrix products, on_device(): jnp.dot(lax.all_gather(tokens, 'seq', axis=0, tiled=True), paired, prefer...  8.26 us
    dot_general x1, matrix products, project_down(): lax.dot_general(hidden, weight, (((1,), (1,)), ((), ())), preferred_eleme...  6.04 us
  transfers between devices with their start and end apart: 1, of which 1 were waited for; matrix products, arithmetic and copies ran while one was open for 0% of the time, Pallas kernels for 0%

profile of v1, /device:TPU:0, one launch (start us, length us, event | category | flops | bytes accessed | tf_op | source)
XLA Modules:
  0.0 146.0 jit_solution(3553491815296364192)
XLA Ops:
  6.5 0.0 all-gather.4.cloned.1.call-start
  6.5 24.8 %all-gather.1 = bf16[16,4,4096]{2,1,0:T(4,128)(2,1)S(1)} all-gather(bf16[1,4,4096]{2,1,0:T(4,128)(2,1)} %bitcast.8), channel_id=1, replica_groups=mesh['seq'=16,'fsdp'=2] {'seq'}, dimensions={0}, use_global_device_ids=true | all-gather | bytes 557056 | tf_op jit(solution)/shard_map/all_gather | solution.py:22
  31.3 0.1 reshape.2
  31.5 0.0 copy-start
  31.5 8.3 %fusion.4 = f32[64,2048]{1,0:T(8,128)} fusion(bf16[64,4096]{1,0:T(8,128)(2,1)S(1)} %reshape.2, bf16[4096,1024]{1,0:T(8,128)(2,1)} %param.6, bf16[4096,1024]{1,0:T(8,128)(2,1)} %param.5), kind=kOutput, calls=%fused_computation.4 | convolution fusion | flops 1107296256 | bytes 17825792 | tf_op jit(solution)/shard_map/dot_general | solution.py:21
  39.7 0.0 all-gather.4.cloned.1.call-update
  39.8 0.0 copy-done
  39.8 0.6 dynamic-slice
  41.0 17.4 %all-gather.4.cloned.1.call-done = f32[128,2048]{1,0:T(8,128)} async-done(((f32[64,2048]{1,0:T(8,128)}), f32[128,2048]{1,0:T(8,128)}) %all-gather.4.cloned.1.call-update) | async-done | bytes 1048592 | tf_op jit(solution)/shard_map/all_gather | solution.py:9
  58.4 1.3 reduce_sum.9
  59.8 6.0 %fusion.8 = f32[64,4096]{1,0:T(8,128)S(1)} fusion(bf16[4096,1024]{1,0:T(8,128)(2,1)} %param.7, f32[64,2048]{1,0:T(8,128)S(1)} %reduce_sum.9), kind=kOutput, calls=%fused_computation.7 | convolution fusion | flops 537264128 | bytes 9961472 | tf_op jit(solution)/shard_map/dot_general | solution.py:13
  65.8 72.7 %all-reduce.2 = bf16[64,4096]{1,0:T(8,128)(2,1)S(1)} all-reduce(f32[64,4096]{1,0:T(8,128)S(1)} %fusion.8), channel_id=3, replica_groups=mesh['seq'=16,'fsdp'=2] {'seq'}, use_global_device_ids=true, to_apply=%region_1.2.clone | all-reduce | flops 262144 | bytes 1572864
  138.5 0.6 dynamic-slice_convert_fusion
Async XLA Ops:
  6.5 51.9 %all-gather.4.cloned.1.call-start = ((), (), s32[]{:S(2)}) async-start(), calls=%async_computation | async-start | bytes 1572864 | tf_op jit(solution)/shard_map/all_gather | solution.py:9
  31.5 8.3 %copy-start = (u32[32]{0:T(128)S(1)}, u32[32]{0:T(128)}, u32[]{:S(2)}) copy-start(u32[32]{0:T(128)} %constant.8) | copy-start | bytes 388
Sparse Core Ops, SparseCore 0:
  39.9 18.5 all-gather.3
